TPU v7x, 32 devices: a whole 2x2x4 slice. The times are simulated.
32 devices in a mesh: tm: 4 (over y, x), space: 8 (over z, core).
Axes of the slice: x: 2, y: 2, z: 4, core: 2. Of those that a mesh axis runs over, the one named last changes fastest.
Arguments:
- hidden_in: bfloat16 [8, 16, 32, 5120], P('tm', 'space'), may hold values from -6 to 6
- queries: bfloat16 [8, 16, 32, 5120], P('tm', 'space'), may hold values from -250 to 250
- keys: bfloat16 [8, 16, 32, 5120], P('tm', 'space'), may hold values from -250 to 250
- values: bfloat16 [8, 16, 32, 5120], P('tm', 'space'), may hold values from -6 to 6
- query_gain: float32 [5120], replicated, may hold values from 0.5 to 3
- key_gain: float32 [5120], replicated, may hold values from 0.5 to 3
- reach_time: int32 [40], replicated, may hold values from 0 to 1
- reach_rows: int32 [40], replicated, may hold values from 0 to 1
- reach_cols: int32 [40], replicated, may hold values from 0 to 2
- out_weight: bfloat16 [5120, 5120], P('space', 'tm'), may hold values from -0.25 to 0.25
- gate: float32 [5120], replicated, may hold values from -1.5 to 1.5
Outputs:
- output: bfloat16 [8, 16, 32, 5120], P('tm', 'space')
All inputs are finite; a program needn't handle non-finite values.
Results may differ from a plain program's by a relative error of at most 0.013.
The roundings to bfloat16 on the way count: a program that leaves them out, or rounds other values in their place, can miss the bound.
Values may be sent and summed in bfloat16 or wider, within the bound.
A program may use at most 128 MiB of HBM per device.

v0:
```python
import jax
import jax.numpy as jnp
from jax import lax
from jax.sharding import PartitionSpec as P

TW = 8


def passed_along(block, axis, distance):
    devices = range(lax.axis_size(axis))
    route = [(i - distance, i) for i in devices if i - distance in devices]
    return lax.ppermute(block, axis, route)


def normalize(source, gain):
    values_f = source.astype(jnp.float32)
    mean_square = jnp.mean(values_f * values_f, axis=-1, keepdims=True)
    return (values_f * lax.rsqrt(mean_square + 1e-06) * gain).astype(jnp.bfloat16)


def attend(
    query_block,
    key_region,
    value_region,
    first_frame,
    first_row,
    frame_count,
    row_count,
    reach_time,
    reach_rows,
    reach_cols,
):
    frames_here, rows_here, columns, inner = query_block.shape
    head_count = reach_time.shape[0]
    head_width = inner // head_count
    query_flat = query_block.reshape(-1, head_count, head_width)
    key_flat = key_region.reshape(-1, head_count, head_width)
    value_flat = value_region.reshape(-1, head_count, head_width)
    frame_q = first_frame + jnp.arange(frames_here, dtype=jnp.int32)
    frame_k = first_frame - 1 + jnp.arange(frames_here + 2, dtype=jnp.int32)
    row_q = first_row + jnp.arange(rows_here, dtype=jnp.int32)
    row_k = first_row - 1 + jnp.arange(rows_here + 2, dtype=jnp.int32)
    tiles = jnp.arange(columns, dtype=jnp.int32) // TW
    query_shape = (frames_here, rows_here, columns)
    key_shape = (frames_here + 2, rows_here + 2, columns)
    query_frame = jnp.broadcast_to(frame_q[:, None, None], query_shape).reshape(-1)
    query_row = jnp.broadcast_to(row_q[None, :, None], query_shape).reshape(-1)
    query_tile = jnp.broadcast_to(tiles[None, None, :], query_shape).reshape(-1)
    key_frame = jnp.broadcast_to(frame_k[:, None, None], key_shape).reshape(-1)
    key_row = jnp.broadcast_to(row_k[None, :, None], key_shape).reshape(-1)
    key_tile = jnp.broadcast_to(tiles[None, None, :], key_shape).reshape(-1)
    frame_gap = jnp.abs(query_frame[:, None] - key_frame[None, :])
    row_gap = jnp.abs(query_row[:, None] - key_row[None, :])
    tile_gap = jnp.abs(query_tile[:, None] - key_tile[None, :])
    inside = (key_frame >= 0) & (key_frame < frame_count) & (key_row >= 0) & (key_row < row_count)
    allowed = (frame_gap[None] <= reach_time[:, None, None]) & (
        row_gap[None] <= reach_rows[:, None, None]
    )
    allowed = allowed & (tile_gap[None] <= reach_cols[:, None, None]) & inside[None, None, :]
    scores = jnp.einsum(
        "qhd,khd->hqk", query_flat, key_flat, preferred_element_type=jnp.float32
    ) * head_width ** (-0.5)
    masked = jnp.where(allowed, scores, -jnp.inf)
    row_peak = jnp.max(masked, axis=2, keepdims=True)
    weights = jnp.exp(masked - row_peak)
    totals = jnp.sum(weights, axis=2, keepdims=True)
    rounded = weights.astype(jnp.bfloat16)
    mixed = jnp.einsum("hqk,khd->qhd", rounded, value_flat, preferred_element_type=jnp.float32)
    mixed = mixed / jnp.transpose(totals, (1, 0, 2))
    return mixed.reshape(mixed.shape[0], inner).astype(jnp.bfloat16)


def shards(
    hidden_in,
    queries,
    keys,
    values,
    query_gain,
    key_gain,
    reach_time,
    reach_rows,
    reach_cols,
    out_weight,
    gate,
):
    frames_here, rows_here, columns, inner = queries.shape
    width = hidden_in.shape[3]
    query_norm = normalize(queries, query_gain)
    key_norm = normalize(keys, key_gain)
    stacked = jnp.stack([key_norm, values])
    below_frame = passed_along(stacked[:, -1:], "tm", 1)
    above_frame = passed_along(stacked[:, :1], "tm", -1)
    framed = jnp.concatenate([below_frame, stacked, above_frame], axis=1)
    below_rows = passed_along(framed[:, :, -1:], "space", 1)
    above_rows = passed_along(framed[:, :, :1], "space", -1)
    region = jnp.concatenate([below_rows, framed, above_rows], axis=2)
    first_frame = lax.axis_index("tm") * frames_here
    first_row = lax.axis_index("space") * rows_here
    frame_count = frames_here * lax.axis_size("tm")
    row_count = rows_here * lax.axis_size("space")
    attention = attend(
        query_norm,
        region[0],
        region[1],
        first_frame,
        first_row,
        frame_count,
        row_count,
        reach_time,
        reach_rows,
        reach_cols,
    )
    token_count = attention.shape[0]
    gathered_rows = lax.all_gather(out_weight, "space", axis=0, tiled=True)
    group_terms = jnp.dot(
        lax.all_gather(attention, "tm", axis=0, tiled=True),
        gathered_rows,
        preferred_element_type=jnp.float32,
    )
    branch = lax.all_to_all(group_terms, "tm", split_axis=0, concat_axis=1, tiled=True)
    residual = hidden_in.reshape(token_count, width).astype(jnp.float32)
    output = (residual + gate * branch).astype(jnp.bfloat16)
    return output.reshape(frames_here, rows_here, columns, width)


def solution(mesh):
    in_specs = (
        P("tm", "space", None, None),
        P("tm", "space", None, None),
        P("tm", "space", None, None),
        P("tm", "space", None, None),
        P(),
        P(),
        P(),
        P(),
        P(),
        P("space", "tm"),
        P(),
    )
    out_specs = P("tm", "space", None, None)
    return jax.shard_map(shards, mesh=mesh, in_specs=in_specs, out_specs=out_specs, check_vma=False)
```

profile of v0, /device:TPU:0, one launch (start us, length us, event | category | flops | bytes accessed | tf_op | source)
XLA Modules:
  0.0 403.5 jit_solution(15969228863281141837)
XLA Ops:
  6.5 1.8 fusion.10
  8.3 1.7 fusion.22
  10.0 1.7 fusion.21
  11.8 5.9 %collective-permute-start = (bf16[2,1,2,32,5120]{4,3,2,1,0:T(8,128)(2,1)}, bf16[2,1,2,32,5120]{4,3,2,1,0:T(8,128)(2,1)}, u32[]{:S(2)}, u32[]{:S(2)}) collective-permute-start(bf16[2,1,2,32,5120]{4,3,2,1,0:T(8,128)(2,1)} %get-tuple-element.9), channel_id=1, source_target_pairs={{0,8},{8,16},{16,24},{1,9},{9,17},{17,25},{2,10},{10,18},{18,26},{... | collective-permute-start | bytes 3932168 | tf_op jit(solution)/shard_map/ppermute | solution.py:12
  17.7 1.3 collective-permute-start.1
  19.0 0.1 broadcast_in_dim.20
  19.1 0.1 sub.92
  19.2 0.1 broadcast_in_dim.19
  19.3 0.1 sub.89
  19.4 25.6 %collective-permute-done = bf16[2,1,2,32,5120]{4,3,2,1,0:T(8,128)(2,1)} collective-permute-done((bf16[2,1,2,32,5120]{4,3,2,1,0:T(8,128)(2,1)}, bf16[2,1,2,32,5120]{4,3,2,1,0:T(8,128)(2,1)}, u32[]{:S(2)}, u32[]{:S(2)}) %collective-permute-start) | collective-permute-done | bytes 1310752 | tf_op jit(solution)/shard_map/ppermute | solution.py:12
  45.0 30.0 %collective-permute-done.1 = bf16[2,1,2,32,5120]{4,3,2,1,0:T(8,128)(2,1)} collective-permute-done((bf16[2,1,2,32,5120]{4,3,2,1,0:T(8,128)(2,1)}, bf16[2,1,2,32,5120]{4,3,2,1,0:T(8,128)(2,1)}, u32[]{:S(2)}, u32[]{:S(2)}) %collective-permute-start.1) | collective-permute-done | bytes 1310752 | tf_op jit(solution)/shard_map/ppermute | solution.py:12
  75.0 2.8 pad_maximum_fusion.1
  77.8 0.0 copy-start.4
  77.8 2.8 fusion.25
  80.6 2.7 collective-permute-start.2
  83.4 1.3 collective-permute-start.3
  84.7 0.1 sub.98
  84.8 0.1 sub.96
  84.8 0.1 broadcast_in_dim.18
  84.9 0.1 sub.86
  85.0 0.1 broadcast_in_dim.17
  85.1 0.1 sub.83
  85.2 1.7 fusion.13
  86.9 1.7 fusion.15
  88.6 1.3 copy.20
  89.9 0.1 subtract_abs_fusion.2
  90.0 0.1 subtract_abs_fusion
  90.1 0.7 collective-permute-done.3
  90.9 8.9 %pad_maximum_fusion = bf16[2,4,4,32,5120]{4,3,2,1,0:T(8,128)(2,1)} fusion(bf16[2,4,1,32,5120]{4,3,2,1,0:T(8,128)(2,1)} %collective-permute-done.3, bf16[2,1,2,32,5120]{4,3,2,1,0:T(8,128)(2,1)} %collective-permute-done.1, bf16[1,2,2,32,5120]{4,3,2,1,0:T(8,128)(2,1)S(1)} %bitcast.35, bf16[1,2,2,32,5120]{4,3,2,1,0:T(8,128)(2,1)S(1)} %fusion.22, ...), kind=kLoop, calls=%fused_computation | loop fusion | flops 26214400 | bytes 20971520 | tf_op jit(solution)/shard_map/concatenate | solution.py:96
  99.8 9.1 %fusion.24 = (bf16[1,4,4,32,5120]{4,3,2,1,0:T(8,128)(2,1)}, bf16[1,4,4,32,5120]{4,3,2,1,0:T(8,128)(2,1)}) fusion(bf16[2,4,4,32,5120]{4,3,2,1,0:T(8,128)(2,1)} %pad_maximum_fusion), kind=kLoop, calls=%fused_computation.44 | loop fusion | bytes 20971520 | tf_op jit(solution)/shard_map/slice | solution.py:104
  108.9 4.1 %copy.21 = bf16[64,8,40,128]{3,2,1,0:T(8,128)(2,1)S(1)} copy(bf16[64,8,40,128]{3,1,2,0:T(8,128)(2,1)} %bitcast.32) | data formatting | bytes 10485760
  113.0 0.0 copy-start.2
  113.0 0.0 copy-start.8
  113.0 1.4 copy.19
  114.5 4.7 %fusion.26 = (f32[40,128]{1,0:T(8,128)S(1)}, f32[40,128,512]{2,1,0:T(8,128)S(1)}) fusion(bf16[512,40,128]{2,1,0:T(8,128)(2,1)S(1)} %bitcast.38, bf16[128,40,128]{2,1,0:T(8,128)(2,1)S(1)} %bitcast.41, pred[512]{0:T(512)(128)(4,1)S(1)} %compare_and_fusion, s32[40]{0:T(128)S(1)} %copy-done.6, s32[128,512]{1,0:T(8,128)S(1)} %get-tuple-element.13, ...), kind=kOutput, calls=%fused_computation.46 | convolution fusion | flops 694676480 | bytes 17847264 | tf_op jit(solution)/shard_map/qhd,khd->hqk/dot_general | solution.py:60
  119.2 2.4 fusion
  121.7 1.5 copy-done.1
  123.2 7.1 %fusion.16 = bf16[128,40,128]{0,2,1:T(8,128)(2,1)} fusion(f32[40,128,512]{2,1,0:T(8,128)} %copy-done.1, f32[40,128]{1,0:T(8,128)S(1)} %get-tuple-element.11, bf16[512,40,128]{2,1,0:T(8,128)(2,1)S(1)} %bitcast.37, f32[128,40]{0,1:T(8,128)S(1)} %bitcast.43), kind=kOutput, calls=%fused_computation.24 | convolution fusion | flops 677642240 | bytes 17080320 | tf_op jit(solution)/shard_map/hqk,khd->qhd/dot_general | solution.py:68
  130.3 0.0 all-gather.3.cloned.1.call-update
  130.3 0.0 all-gather.5.cloned.1.call-start
  130.3 0.7 all-gather.5.cloned.1.call-update
  131.1 86.1 %all-gather.3.cloned.1.call-done = bf16[512,5120]{0,1:T(8,128)(2,1)} async-done(((bf16[128,5120]{0,1:T(8,128)(2,1)}), bf16[512,5120]{0,1:T(8,128)(2,1)}) %all-gather.3.cloned.1.call-update) | async-done | bytes 5242896 | tf_op jit(solution)/shard_map/all_gather | solution.py:116
  217.2 122.7 %all-gather.5.cloned.1.call-done = bf16[5120,1280]{1,0:T(8,128)(2,1)} async-done(((bf16[640,1280]{1,0:T(8,128)(2,1)}), bf16[5120,1280]{1,0:T(8,128)(2,1)}) %all-gather.5.cloned.1.call-update) | async-done | bytes 13107216 | tf_op jit(solution)/shard_map/all_gather | solution.py:114
  339.9 11.5 %fusion.27 = f32[512,1280]{1,0:T(8,128)S(1)} fusion(bf16[512,5120]{0,1:T(8,128)(2,1)} %all-gather.3.cloned.1.call-done, bf16[5120,1280]{1,0:T(8,128)(2,1)} %all-gather.5.cloned.1.call-done), kind=kOutput, calls=%fused_computation.47 | convolution fusion | flops 6710886400 | bytes 20971520 | tf_op jit(solution)/shard_map/dot_general | solution.py:115
  351.4 34.9 %all_to_all.19 = f32[4,128,1280]{2,1,0:T(8,128)S(1)} all-to-all(f32[4,128,1280]{2,1,0:T(8,128)S(1)} %bitcast.40), channel_id=1, replica_groups=mesh['tm'=4,'space'=8] {'tm'}, dimensions={0} | all-to-all | bytes 5242880 | tf_op jit(solution)/shard_map/all_to_all | solution.py:120
  386.2 3.2 copy.18
  389.4 4.1 %all_to_all.17 = f32[2,2,32,5120]{3,2,1,0:T(8,128)} reshape(f32[128,4,1280]{2,1,0:T(4,128)} %copy.18) | data formatting | bytes 5242880 | tf_op jit(solution)/shard_map/all_to_all | solution.py:120
  393.5 3.1 add_convert_fusion
  (31 shorter events, 0.1 us)
Async XLA Ops:
  6.5 3.5 copy-start
  6.5 210.6 %all-gather.3.cloned.1.call-start = ((), (), s32[]{:S(2)}) async-start(), calls=%async_computation.1 | async-start | bytes 6553600 | tf_op jit(solution)/shard_map/all_gather | solution.py:116
  11.8 33.2 %collective-permute-start = (bf16[2,1,2,32,5120]{4,3,2,1,0:T(8,128)(2,1)}, bf16[2,1,2,32,5120]{4,3,2,1,0:T(8,128)(2,1)}, u32[]{:S(2)}, u32[]{:S(2)}) collective-permute-start(bf16[2,1,2,32,5120]{4,3,2,1,0:T(8,128)(2,1)} %get-tuple-element.9), channel_id=1, source_target_pairs={{0,8},{8,16},{16,24},{1,9},{9,17},{17,25},{2,10},{10,18},{18,26},{... | collective-permute-start | bytes 3932168 | tf_op jit(solution)/shard_map/ppermute | solution.py:12
  17.7 57.3 %collective-permute-start.1 = (bf16[2,1,2,32,5120]{4,3,2,1,0:T(8,128)(2,1)}, bf16[2,1,2,32,5120]{4,3,2,1,0:T(8,128)(2,1)}, u32[]{:S(2)}, u32[]{:S(2)}) collective-permute-start(bf16[2,1,2,32,5120]{4,3,2,1,0:T(8,128)(2,1)} %get-tuple-element.10), channel_id=1, source_target_pairs={{8,0},{16,8},{24,16},{9,1},{17,9},{25,17},{10,2},{18,10},{26,18},{... | collective-permute-start | bytes 3932168 | tf_op jit(solution)/shard_map/ppermute | solution.py:12
  77.8 9.0 %copy-start.4 = (f32[5120]{0:T(1024)S(1)}, f32[5120]{0:T(1024)}, u32[]{:S(2)}) copy-start(f32[5120]{0:T(1024)} %param.15) | copy-start | bytes 61444
  80.6 9.5 %collective-permute-start.2 = (bf16[2,4,1,32,5120]{4,3,2,1,0:T(8,128)(2,1)}, bf16[2,4,1,32,5120]{4,3,2,1,0:T(8,128)(2,1)}, u32[]{:S(2)}, u32[]{:S(2)}) collective-permute-start(bf16[2,4,1,32,5120]{4,3,2,1,0:T(8,128)(2,1)} %get-tuple-element.7), channel_id=1, source_target_pairs={{0,1},{1,2},{2,3},{3,4},{4,5},{5,6},{6,7},{8,9},{9,10},{10,11},{11... | collective-permute-start | bytes 7864328 | tf_op jit(solution)/shard_map/ppermute | solution.py:12
  83.4 7.5 %collective-permute-start.3 = (bf16[2,4,1,32,5120]{4,3,2,1,0:T(8,128)(2,1)}, bf16[2,4,1,32,5120]{4,3,2,1,0:T(8,128)(2,1)}, u32[]{:S(2)}, u32[]{:S(2)}) collective-permute-start(bf16[2,4,1,32,5120]{4,3,2,1,0:T(8,128)(2,1)} %get-tuple-element.8), channel_id=1, source_target_pairs={{1,0},{2,1},{3,2},{4,3},{5,4},{6,5},{7,6},{9,8},{10,9},{11,10},{12... | collective-permute-start | bytes 7864328 | tf_op jit(solution)/shard_map/ppermute | solution.py:12
  108.9 4.1 %slice-start = ((s8[5242880]{0:T(1024)(128)(4,1)}), s8[4194304]{0:T(1024)(128)(4,1)S(1)}, s32[]{:S(2)}) async-start(s8[5242880]{0:T(1024)(128)(4,1)} %bitcast.29), calls=%async_computation.3 | async-start | bytes 8388608
  108.9 4.1 %slice-start.1 = ((s8[5242880]{0:T(1024)(128)(4,1)}), s8[1048576]{0:T(1024)(128)(4,1)S(1)}, s32[]{:S(2)}) async-start(s8[5242880]{0:T(1024)(128)(4,1)} %bitcast.29), calls=%async_computation.4 | async-start | bytes 2097152
  113.0 1.5 copy-start.2
  113.0 1.5 copy-start.6
  113.0 1.5 copy-start.7
  113.0 1.5 copy-start.8
  119.2 4.0 copy-start.1
  130.3 209.6 %all-gather.5.cloned.1.call-start = ((), (), s32[]{:S(2)}) async-start(), calls=%async_computation.2 | async-start | bytes 14745600 | tf_op jit(solution)/shard_map/all_gather | solution.py:114
  389.4 4.1 %copy-start.3 = (bf16[2,2,32,5120]{3,2,1,0:T(8,128)(2,1)S(1)}, bf16[2,2,32,5120]{3,2,1,0:T(8,128)(2,1)}, u32[]{:S(2)}) copy-start(bf16[2,2,32,5120]{3,2,1,0:T(8,128)(2,1)} %param.11) | copy-start | bytes 3932164
  389.4 4.1 %copy-start.5 = (f32[5120]{0:T(1024)S(1)}, f32[5120]{0:T(1024)}, u32[]{:S(2)}) copy-start(f32[5120]{0:T(1024)} %param.21) | copy-start | bytes 61444
Sparse Core Ops, SparseCore 0:
  130.4 86.7 all-gather.2
  218.8 120.9 all-gather.4
where the time goes:
time: 404 us
  waiting for transfers between devices  266 us (66%)
  blocking collectives  34.9 us (9%)
  local copies, waits for them, and re-layouts  28.3 us (7%)
  other arithmetic  26.2 us (6%)
  matrix products  23.3 us (6%)
  between operations  13.7 us (3%)
  starting transfers between devices  11.3 us (3%)
    all_gather x1, waiting for transfers between devices, shards(): gathered_rows = lax.all_gather(out_weight, 'space', axis=0, tiled=True)  123 us
    all_gather x1, waiting for transfers between devices, shards(): lax.all_gather(attention, 'tm', axis=0, tiled=True)  86.1 us
    ppermute x4, waiting for transfers between devices, passed_along(): return lax.ppermute(block, axis, route)  56.4 us
    all_to_all x1, blocking collectives, shards(): lax.all_to_all(group_terms, 'tm', split_axis=0, concat_axis=1, tiled=True)  34.9 us
    dot_general x1, matrix products, shards(): jnp.dot(lax.all_gather(attention, 'tm', axis=0, tiled=True), gathered_row...  11.5 us
    ppermute x4, starting transfers between devices, passed_along(): return lax.ppermute(block, axis, route)  11.3 us
    slice x1, local copies, waits for them, and re-layouts, shards(): region[1]  9.06 us
    concatenate x1, other arithmetic, shards(): region = jnp.concatenate([below_rows, framed, above_rows], axis=2)  8.94 us
  transfers between devices with their start and end apart: 6, of which 5 were waited for; matrix products, arithmetic and copies ran while one was open for 1% of the time, Pallas kernels for 0%

commit v1 on v0

--- a/solution.py
+++ b/solution.py
@@ -111,7 +111,16 @@
         reach_cols,
     )
     token_count = attention.shape[0]
-    gathered_rows = lax.all_gather(out_weight, "space", axis=0, tiled=True)
+    parts_n = lax.psum(1, "space")
+    seen_now = sorted(((b, (b + 1) % parts_n) for b in range(parts_n)))
+    carry_in = out_weight
+    leaves = [carry_in]
+    for ii in tuple(range(1, parts_n)):
+        carry_in = lax.ppermute(carry_in, "space", seen_now)
+        leaves.insert(0, carry_in)
+    x_next = jnp.concatenate(leaves, axis=0)
+    then = lax.axis_index("space") + 1
+    gathered_rows = jnp.roll(x_next, shift=then * out_weight.shape[0], axis=0)
     group_terms = jnp.dot(
         lax.all_gather(attention, "tm", axis=0, tiled=True),
         gathered_rows,

time: 404 us -> 332 us (0.82)
  waiting for transfers between devices: 266 us -> 158 us
  local copies, waits for them, and re-layouts: 28.3 us -> 65.6 us
  blocking collectives: 34.9 us -> 25.9 us
    all_gather x1 -> x0, waiting for transfers between devices: 123 us -> none  [shards(): gathered_rows = lax.all_gather(out_weight, 'space', axis=0, tiled=True)]
    ppermute x0 -> x7, waiting for transfers between devices: none -> 102 us  [shards(): carry_in = lax.ppermute(carry_in, 'space', seen_now)]
    all_gather x1, waiting for transfers between devices: 86.1 us -> 0.01 us  [shards(): lax.all_gather(attention, 'tm', axis=0, tiled=True)]
    unnamed x25 -> x36, local copies, waits for them, and re-layouts: 8.41 us -> 46 us
    all_to_all x1, blocking collectives: 34.9 us -> 25.9 us  [shards(): lax.all_to_all(group_terms, 'tm', split_axis=0, concat_axis=1, tiled=True)]
  transfers between devices with their start and end apart: 6 -> 12, of which waited for: 5 -> 7; matrix products, arithmetic and copies ran while one was open for 1% -> 28% of each run, Pallas kernels for 0% -> 0%
where the time goes in v1:
time: 332 us; the launch traced here: 331 us
  waiting for transfers between devices  158 us (48%)
  local copies, waits for them, and re-layouts  65.6 us (20%)
  other arithmetic  27.8 us (8%)
  matrix products  26 us (8%)
  blocking collectives  25.9 us (8%)
  starting transfers between devices  13.9 us (4%)
  between operations  13.6 us (4%)
    ppermute x7, waiting for transfers between devices, shards(): carry_in = lax.ppermute(carry_in, 'space', seen_now)  102 us
    ppermute x4, waiting for transfers between devices, passed_along(): return lax.ppermute(block, axis, route)  55.6 us
    unnamed x36, local copies, waits for them, and re-layouts  46 us
    all_to_all x1, blocking collectives, shards(): lax.all_to_all(group_terms, 'tm', split_axis=0, concat_axis=1, tiled=True)  25.9 us
    ppermute x4, starting transfers between devices, passed_along(): return lax.ppermute(block, axis, route)  13.5 us
    dot_general x1, matrix products, shards(): jnp.dot(lax.all_gather(attention, 'tm', axis=0, tiled=True), gathered_row...  11.5 us
    dot_general x1, matrix products, attend(): jnp.einsum('hqk,khd->qhd', rounded, value_flat, preferred_element_type=jn...  9.79 us
    slice x1, local copies, waits for them, and re-layouts, shards(): region[1]  9.06 us
  transfers between devices with their start and end apart: 12, of which 7 were waited for; matrix products, arithmetic and copies ran while one was open for 28% of the time, Pallas kernels for 0%

profile of v1, /device:TPU:0, one launch (start us, length us, event | category | flops | bytes accessed | tf_op | source)
XLA Modules:
  0.0 331.0 jit_solution(7820716988760322531)
XLA Ops:
  6.5 1.8 fusion.12
  8.3 1.7 fusion.24
  10.0 3.0 fusion.23
  13.1 5.9 %collective-permute-start = (bf16[2,1,2,32,5120]{4,3,2,1,0:T(8,128)(2,1)}, bf16[2,1,2,32,5120]{4,3,2,1,0:T(8,128)(2,1)}, u32[]{:S(2)}, u32[]{:S(2)}) collective-permute-start(bf16[2,1,2,32,5120]{4,3,2,1,0:T(8,128)(2,1)} %get-tuple-element.9), channel_id=1, source_target_pairs={{0,8},{8,16},{16,24},{1,9},{9,17},{17,25},{2,10},{10,18},{18,26},{... | collective-permute-start | bytes 3932168 | tf_op jit(solution)/shard_map/ppermute | solution.py:12
  19.0 1.3 collective-permute-start.1
  20.7 25.6 %collective-permute-done = bf16[2,1,2,32,5120]{4,3,2,1,0:T(8,128)(2,1)} collective-permute-done((bf16[2,1,2,32,5120]{4,3,2,1,0:T(8,128)(2,1)}, bf16[2,1,2,32,5120]{4,3,2,1,0:T(8,128)(2,1)}, u32[]{:S(2)}, u32[]{:S(2)}) %collective-permute-start) | collective-permute-done | bytes 1310752 | tf_op jit(solution)/shard_map/ppermute | solution.py:12
  46.3 30.0 %collective-permute-done.1 = bf16[2,1,2,32,5120]{4,3,2,1,0:T(8,128)(2,1)} collective-permute-done((bf16[2,1,2,32,5120]{4,3,2,1,0:T(8,128)(2,1)}, bf16[2,1,2,32,5120]{4,3,2,1,0:T(8,128)(2,1)}, u32[]{:S(2)}, u32[]{:S(2)}) %collective-permute-start.1) | collective-permute-done | bytes 1310752 | tf_op jit(solution)/shard_map/ppermute | solution.py:12
  76.3 2.8 pad_maximum_fusion.1
  79.2 2.8 fusion.28
  82.0 5.0 %collective-permute-start.2 = (bf16[2,4,1,32,5120]{4,3,2,1,0:T(8,128)(2,1)}, bf16[2,4,1,32,5120]{4,3,2,1,0:T(8,128)(2,1)}, u32[]{:S(2)}, u32[]{:S(2)}) collective-permute-start(bf16[2,4,1,32,5120]{4,3,2,1,0:T(8,128)(2,1)} %get-tuple-element.7), channel_id=1, source_target_pairs={{0,1},{1,2},{2,3},{3,4},{4,5},{5,6},{6,7},{8,9},{9,10},{10,11},{11... | collective-permute-start | bytes 7864328 | tf_op jit(solution)/shard_map/ppermute | solution.py:12
  87.0 1.3 collective-permute-start.3
  88.8 1.7 fusion.15
  90.5 20.2 %collective-permute-done.5 = bf16[640,1280]{1,0:T(8,128)(2,1)} collective-permute-done((bf16[640,1280]{1,0:T(8,128)(2,1)}, bf16[640,1280]{1,0:T(8,128)(2,1)}, u32[]{:S(2)}, u32[]{:S(2)}) %collective-permute-start.5) | collective-permute-done | bytes 1638432 | tf_op jit(solution)/shard_map/ppermute | solution.py:119
  110.7 1.7 fusion.17
  112.5 1.3 copy.20
  114.0 33.5 %collective-permute-done.6 = bf16[640,1280]{1,0:T(8,128)(2,1)} collective-permute-done((bf16[640,1280]{1,0:T(8,128)(2,1)}, bf16[640,1280]{1,0:T(8,128)(2,1)}, u32[]{:S(2)}, u32[]{:S(2)}) %collective-permute-start.6) | collective-permute-done | bytes 1638432 | tf_op jit(solution)/shard_map/ppermute | solution.py:119
  147.5 9.0 %pad_maximum_fusion = bf16[2,4,4,32,5120]{4,3,2,1,0:T(8,128)(2,1)} fusion(bf16[2,4,1,32,5120]{4,3,2,1,0:T(8,128)(2,1)} %collective-permute-done.3, bf16[2,1,2,32,5120]{4,3,2,1,0:T(8,128)(2,1)} %collective-permute-done.1, bf16[1,2,2,32,5120]{4,3,2,1,0:T(8,128)(2,1)S(1)} %bitcast.32, bf16[1,2,2,32,5120]{4,3,2,1,0:T(8,128)(2,1)S(1)} %fusion.24, ...), kind=kLoop, calls=%fused_computation.2 | loop fusion | flops 26214400 | bytes 20971520 | tf_op jit(solution)/shard_map/concatenate | solution.py:96
  156.5 9.1 %fusion.27 = (bf16[1,4,4,32,5120]{4,3,2,1,0:T(8,128)(2,1)}, bf16[1,4,4,32,5120]{4,3,2,1,0:T(8,128)(2,1)}) fusion(bf16[2,4,4,32,5120]{4,3,2,1,0:T(8,128)(2,1)} %pad_maximum_fusion), kind=kLoop, calls=%fused_computation.63 | loop fusion | bytes 20971520 | tf_op jit(solution)/shard_map/slice | solution.py:104
  165.5 6.4 %copy.19 = bf16[64,8,40,128]{3,2,1,0:T(8,128)(2,1)} copy(bf16[64,8,40,128]{3,1,2,0:T(8,128)(2,1)} %bitcast.29) | data formatting | bytes 10485760
  172.0 1.4 copy.21
  173.7 4.7 %fusion.29 = (f32[40,128]{1,0:T(8,128)S(1)}, f32[40,128,512]{2,1,0:T(8,128)S(1)}) fusion(bf16[512,40,128]{2,1,0:T(8,128)(2,1)S(1)} %bitcast.35, bf16[128,40,128]{2,1,0:T(8,128)(2,1)S(1)} %bitcast.39, pred[512]{0:T(512)(128)(4,1)S(1)} %compare_and_fusion, s32[40]{0:T(128)S(1)} %copy-done.6, s32[128,512]{1,0:T(8,128)S(1)} %get-tuple-element.13, ...), kind=kOutput, calls=%fused_computation.65 | convolution fusion | flops 694676480 | bytes 17847264 | tf_op jit(solution)/shard_map/qhd,khd->hqk/dot_general | solution.py:60
  178.5 2.4 fusion.2
  180.9 1.5 copy-done.2
  182.4 13.8 %collective-permute-done.8 = bf16[640,1280]{1,0:T(8,128)(2,1)S(1)} collective-permute-done((bf16[640,1280]{1,0:T(8,128)(2,1)}, bf16[640,1280]{1,0:T(8,128)(2,1)S(1)}, u32[]{:S(2)}, u32[]{:S(2)}) %collective-permute-start.8) | collective-permute-done | bytes 1638432 | tf_op jit(solution)/shard_map/ppermute | solution.py:119
  196.2 9.8 %fusion.18 = bf16[128,40,128]{0,2,1:T(8,128)(2,1)} fusion(f32[40,128,512]{2,1,0:T(8,128)} %copy-done.2, f32[40,128]{1,0:T(8,128)S(1)} %get-tuple-element.11, bf16[512,40,128]{2,1,0:T(8,128)(2,1)} %bitcast.34, f32[128,40]{0,1:T(8,128)S(1)} %bitcast.40), kind=kOutput, calls=%fused_computation.26 | convolution fusion | flops 677642240 | bytes 17080320 | tf_op jit(solution)/shard_map/hqk,khd->qhd/dot_general | solution.py:68
  206.0 12.5 %collective-permute-done.9 = bf16[640,1280]{1,0:T(8,128)(2,1)S(1)} collective-permute-done((bf16[640,1280]{1,0:T(8,128)(2,1)S(1)}, bf16[640,1280]{1,0:T(8,128)(2,1)S(1)}, u32[]{:S(2)}, u32[]{:S(2)}) %collective-permute-start.9) | collective-permute-done | bytes 1638432 | tf_op jit(solution)/shard_map/ppermute | solution.py:119
  218.6 22.4 %collective-permute-done.10 = bf16[640,1280]{1,0:T(8,128)(2,1)} collective-permute-done((bf16[640,1280]{1,0:T(8,128)(2,1)S(1)}, bf16[640,1280]{1,0:T(8,128)(2,1)}, u32[]{:S(2)}, u32[]{:S(2)}) %collective-permute-start.10) | collective-permute-done | bytes 1638432 | tf_op jit(solution)/shard_map/ppermute | solution.py:119
  241.0 2.8 constant_dynamic-update-slice_fusion.15
  243.8 1.3 constant_dynamic-update-slice_fusion.14
  245.1 1.3 constant_dynamic-update-slice_fusion.13
  246.4 2.8 constant_dynamic-update-slice_fusion.12
  249.2 2.7 constant_dynamic-update-slice_fusion.11
  251.9 2.8 constant_dynamic-update-slice_fusion.10
  254.6 2.7 constant_dynamic-update-slice_fusion.9
  257.4 2.8 constant_dynamic-update-slice_fusion.8
  260.2 2.7 constant_dynamic-update-slice_fusion.7
  262.9 1.3 constant_dynamic-update-slice_fusion.6
  264.1 1.3 constant_dynamic-update-slice_fusion.5
  265.4 2.7 constant_dynamic-update-slice_fusion.4
  268.1 2.7 constant_dynamic-update-slice_fusion.3
  270.9 2.7 constant_dynamic-update-slice_fusion.2
  273.6 2.7 constant_dynamic-update-slice_fusion.1
  276.3 2.8 constant_dynamic-update-slice_fusion
  279.1 11.5 %fusion = f32[512,1280]{1,0:T(8,128)S(1)} fusion(bf16[512,5120]{0,1:T(8,128)(2,1)} %all-gather.2.cloned.1.call-done, bf16[10240,1280]{1,0:T(8,128)(2,1)} %constant_dynamic-update-slice_fusion, s32[]{:T(128)S(6)} %select_n.29), kind=kOutput, calls=%fused_computation | convolution fusion | flops 6710886400 | bytes 20971524 | tf_op jit(solution)/shard_map/dot_general | solution.py:124
  290.6 25.9 %all_to_all.19 = f32[4,128,1280]{2,1,0:T(8,128)S(1)} all-to-all(f32[4,128,1280]{2,1,0:T(8,128)S(1)} %bitcast.37), channel_id=1, replica_groups=mesh['tm'=4,'space'=8] {'tm'}, dimensions={0} | all-to-all | bytes 5242880 | tf_op jit(solution)/shard_map/all_to_all | solution.py:129
  316.5 1.7 copy.18
  318.2 2.5 all_to_all.17
  320.7 3.5 %add_convert_fusion = bf16[2,2,32,5120]{3,2,1,0:T(8,128)(2,1)} fusion(f32[2,2,32,5120]{3,2,1,0:T(8,128)} %all_to_all.17, bf16[2,2,32,5120]{3,2,1,0:T(8,128)(2,1)} %param.11, f32[5120]{0:T(1024)S(1)} %copy-done.5), kind=kLoop, calls=%fused_computation.27 | loop fusion | flops 2621440 | bytes 5263360 | tf_op jit(solution)/shard_map/convert_element_type | solution.py:131
  (53 shorter events, 1.5 us)
Async XLA Ops:
  6.5 69.8 %copy-start.1 = (bf16[2,2,32,5120]{3,2,1,0:T(8,128)(2,1)S(1)}, bf16[2,2,32,5120]{3,2,1,0:T(8,128)(2,1)}, u32[]{:S(2)}) copy-start(bf16[2,2,32,5120]{3,2,1,0:T(8,128)(2,1)} %param.14) | copy-start | bytes 3932164
  6.5 272.5 %all-gather.2.cloned.1.call-start = ((), (), s32[]{:S(2)}) async-start(), calls=%async_computation.1 | async-start | bytes 6553600 | tf_op jit(solution)/shard_map/all_gather | solution.py:125
  13.1 33.2 %collective-permute-start = (bf16[2,1,2,32,5120]{4,3,2,1,0:T(8,128)(2,1)}, bf16[2,1,2,32,5120]{4,3,2,1,0:T(8,128)(2,1)}, u32[]{:S(2)}, u32[]{:S(2)}) collective-permute-start(bf16[2,1,2,32,5120]{4,3,2,1,0:T(8,128)(2,1)} %get-tuple-element.9), channel_id=1, source_target_pairs={{0,8},{8,16},{16,24},{1,9},{9,17},{17,25},{2,10},{10,18},{18,26},{... | collective-permute-start | bytes 3932168 | tf_op jit(solution)/shard_map/ppermute | solution.py:12
  19.0 57.3 %collective-permute-start.1 = (bf16[2,1,2,32,5120]{4,3,2,1,0:T(8,128)(2,1)}, bf16[2,1,2,32,5120]{4,3,2,1,0:T(8,128)(2,1)}, u32[]{:S(2)}, u32[]{:S(2)}) collective-permute-start(bf16[2,1,2,32,5120]{4,3,2,1,0:T(8,128)(2,1)} %get-tuple-element.10), channel_id=1, source_target_pairs={{8,0},{16,8},{24,16},{9,1},{17,9},{25,17},{10,2},{18,10},{26,18},{... | collective-permute-start | bytes 3932168 | tf_op jit(solution)/shard_map/ppermute | solution.py:12
  20.3 58.8 %collective-permute-start.4 = (bf16[640,1280]{1,0:T(8,128)(2,1)}, bf16[640,1280]{1,0:T(8,128)(2,1)}, u32[]{:S(2)}, u32[]{:S(2)}) collective-permute-start(bf16[640,1280]{1,0:T(8,128)(2,1)} %param.20), channel_id=1, source_target_pairs={{0,1},{1,2},{2,3},{3,4},{4,5},{5,6},{6,7},{7,0},{8,9},{9,10},{10,1... | collective-permute-start | bytes 4915208 | tf_op jit(solution)/shard_map/ppermute | solution.py:119
  79.1 31.6 %copy-start.4 = (f32[5120]{0:T(1024)S(1)}, f32[5120]{0:T(1024)}, u32[]{:S(2)}) copy-start(f32[5120]{0:T(1024)} %param.15) | copy-start | bytes 61444
  79.2 31.6 %collective-permute-start.5 = (bf16[640,1280]{1,0:T(8,128)(2,1)}, bf16[640,1280]{1,0:T(8,128)(2,1)}, u32[]{:S(2)}, u32[]{:S(2)}) collective-permute-start(bf16[640,1280]{1,0:T(8,128)(2,1)} %collective-permute-done.4), channel_id=1, source_target_pairs={{0,1},{1,2},{2,3},{3,4},{4,5},{5,6},{6,7},{7,0},{8,9},{9,10},{10,1... | collective-permute-start | bytes 4915208 | tf_op jit(solution)/shard_map/ppermute | solution.py:119
  82.0 65.5 %collective-permute-start.2 = (bf16[2,4,1,32,5120]{4,3,2,1,0:T(8,128)(2,1)}, bf16[2,4,1,32,5120]{4,3,2,1,0:T(8,128)(2,1)}, u32[]{:S(2)}, u32[]{:S(2)}) collective-permute-start(bf16[2,4,1,32,5120]{4,3,2,1,0:T(8,128)(2,1)} %get-tuple-element.7), channel_id=1, source_target_pairs={{0,1},{1,2},{2,3},{3,4},{4,5},{5,6},{6,7},{8,9},{9,10},{10,11},{11... | collective-permute-start | bytes 7864328 | tf_op jit(solution)/shard_map/ppermute | solution.py:12
  87.0 60.5 %collective-permute-start.3 = (bf16[2,4,1,32,5120]{4,3,2,1,0:T(8,128)(2,1)}, bf16[2,4,1,32,5120]{4,3,2,1,0:T(8,128)(2,1)}, u32[]{:S(2)}, u32[]{:S(2)}) collective-permute-start(bf16[2,4,1,32,5120]{4,3,2,1,0:T(8,128)(2,1)} %get-tuple-element.8), channel_id=1, source_target_pairs={{1,0},{2,1},{3,2},{4,3},{5,4},{6,5},{7,6},{9,8},{10,9},{11,10},{12... | collective-permute-start | bytes 7864328 | tf_op jit(solution)/shard_map/ppermute | solution.py:12
  110.7 36.8 %collective-permute-start.6 = (bf16[640,1280]{1,0:T(8,128)(2,1)}, bf16[640,1280]{1,0:T(8,128)(2,1)}, u32[]{:S(2)}, u32[]{:S(2)}) collective-permute-start(bf16[640,1280]{1,0:T(8,128)(2,1)} %collective-permute-done.5), channel_id=1, source_target_pairs={{0,1},{1,2},{2,3},{3,4},{4,5},{5,6},{6,7},{7,0},{8,9},{9,10},{10,1... | collective-permute-start | bytes 4915208 | tf_op jit(solution)/shard_map/ppermute | solution.py:119
  147.5 25.9 %collective-permute-start.7 = (bf16[640,1280]{1,0:T(8,128)(2,1)}, bf16[640,1280]{1,0:T(8,128)(2,1)}, u32[]{:S(2)}, u32[]{:S(2)}) collective-permute-start(bf16[640,1280]{1,0:T(8,128)(2,1)} %collective-permute-done.6), channel_id=1, source_target_pairs={{0,1},{1,2},{2,3},{3,4},{4,5},{5,6},{6,7},{7,0},{8,9},{9,10},{10,1... | collective-permute-start | bytes 4915208 | tf_op jit(solution)/shard_map/ppermute | solution.py:119
  165.5 6.4 %copy-start = (bf16[1,4,4,32,5120]{4,3,2,1,0:T(8,128)(2,1)S(1)}, bf16[1,4,4,32,5120]{4,3,2,1,0:T(8,128)(2,1)}, u32[]{:S(2)}) copy-start(bf16[1,4,4,32,5120]{4,3,2,1,0:T(8,128)(2,1)} %get-tuple-element.6) | copy-start | bytes 15728644
  172.0 1.7 copy-start.3
  172.0 1.7 copy-start.6
  172.0 1.7 copy-start.7
  172.0 1.8 copy-start.8
  173.4 22.8 %collective-permute-start.8 = (bf16[640,1280]{1,0:T(8,128)(2,1)}, bf16[640,1280]{1,0:T(8,128)(2,1)S(1)}, u32[]{:S(2)}, u32[]{:S(2)}) collective-permute-start(bf16[640,1280]{1,0:T(8,128)(2,1)} %collective-permute-done.7), channel_id=1, source_target_pairs={{0,1},{1,2},{2,3},{3,4},{4,5},{5,6},{6,7},{7,0},{8,9},{9,10},{10,1... | collective-permute-start | bytes 4915208 | tf_op jit(solution)/shard_map/ppermute | solution.py:119
  178.4 4.0 %copy-start.2 = (f32[40,128,512]{2,1,0:T(8,128)}, f32[40,128,512]{2,1,0:T(8,128)S(1)}, u32[]{:S(2)}) copy-start(f32[40,128,512]{2,1,0:T(8,128)S(1)} %get-tuple-element.12) | copy-start | bytes 31457284
  196.2 22.3 %collective-permute-start.9 = (bf16[640,1280]{1,0:T(8,128)(2,1)S(1)}, bf16[640,1280]{1,0:T(8,128)(2,1)S(1)}, u32[]{:S(2)}, u32[]{:S(2)}) collective-permute-start(bf16[640,1280]{1,0:T(8,128)(2,1)S(1)} %collective-permute-done.8), channel_id=1, source_target_pairs={{0,1},{1,2},{2,3},{3,4},{4,5},{5,6},{6,7},{7,0},{8,9},{9,10},{10,1... | collective-permute-start | bytes 4915208 | tf_op jit(solution)/shard_map/ppermute | solution.py:119
  218.6 22.4 %collective-permute-start.10 = (bf16[640,1280]{1,0:T(8,128)(2,1)S(1)}, bf16[640,1280]{1,0:T(8,128)(2,1)}, u32[]{:S(2)}, u32[]{:S(2)}) collective-permute-start(bf16[640,1280]{1,0:T(8,128)(2,1)S(1)} %collective-permute-done.9), channel_id=1, source_target_pairs={{0,1},{1,2},{2,3},{3,4},{4,5},{5,6},{6,7},{7,0},{8,9},{9,10},{10,1... | collective-permute-start | bytes 4915208 | tf_op jit(solution)/shard_map/ppermute | solution.py:119
  316.5 4.2 %copy-start.5 = (f32[5120]{0:T(1024)S(1)}, f32[5120]{0:T(1024)}, u32[]{:S(2)}) copy-start(f32[5120]{0:T(1024)} %param.21) | copy-start | bytes 61444
Sparse Core Ops, SparseCore 0:
  206.2 61.4 all-gather.1
